TPU v7x, 256 devices: a whole 4x4x8 slice. The times are simulated.
256 devices in a mesh: col: 128 (over x, z, y), sec: 2 (over core).
Axes of the slice: x: 4, y: 4, z: 8, core: 2. Of those that a mesh axis runs over, the one named last changes fastest.
Arguments:
- mps: bfloat16 [128, 96, 6, 6, 96], P('col', 'sec'), may hold values from -6 to 6
- ket: bfloat16 [128, 6, 6, 6, 6, 2], P('col'), may hold values from -6 to 6
- left_proj: bfloat16 [128, 96, 96, 6, 6], P('col', 'sec'), may hold values from -0.109375 to 0.109375
- right_proj: bfloat16 [128, 96, 6, 6, 96], P('col', None, None, None, 'sec'), may hold values from -0.109375 to 0.109375
- bond_charge: int32 [128, 96], P('col'), may hold values from 0 to 5
- new_charge: int32 [128, 96], P('col'), may hold values from 0 to 5
- link_charge: int32 [128, 6], P('col'), may hold values from 0 to 2
- vert_charge: int32 [128, 2, 6], P('col'), may hold values from 0 to 2
Outputs:
- new_mps: bfloat16 [128, 96, 6, 6, 96], P('col', 'sec')
- log_norm: float32 [], replicated
All inputs are finite; a program needn't handle non-finite values.
Results may differ from a plain program's by a relative error of at most 0.0064.
Values may be sent and summed in bfloat16 or wider, within the bound.
A program may use at most 192 MiB of HBM per device.

v0:
```python
import functools
import jax
import jax.numpy as jnp
from jax import lax
from jax.sharding import Mesh
from jax.sharding import PartitionSpec as P

COL = ("col_0", "col_1", "col_2")


def from_behind(x, axis, by):
    count = lax.axis_size(axis)
    return lax.ppermute(x, axis, [(i, (i + by) % count) for i in range(count)])


def joined_along(tiles, dim):
    tiles = jnp.moveaxis(tiles, 0, dim)
    shape = tiles.shape
    return tiles.reshape(*shape[:dim], shape[dim] * shape[dim + 1], *shape[dim + 2 :])


def copy_for_each(x, axis):
    count = lax.axis_size(axis)
    return lax.all_to_all(jnp.broadcast_to(x[None], (count, *x.shape)), axis, 0, 0, tiled=True)


def gather_directly(x, axis, dim):
    return joined_along(copy_for_each(x, axis), dim)


def gathered_total(x, axis):
    tiles = lax.all_gather(x, axis)
    return tiles.sum(axis=0)


def one_axis_at_a_time(x, axes):
    return functools.reduce(lax.psum, axes, x)


def absorb(
    mps_site,
    ket_site,
    left_site,
    right_site,
    charge_here,
    charge_next,
    fresh_here,
    fresh_next,
    link_here,
    link_next,
    vertical,
):
    upper = vertical[0]
    lower = vertical[1]
    physical = jnp.arange(ket_site.shape[4], dtype=jnp.int32)
    keep_mps = (
        charge_here[:, None, None, None] + upper[None, :, None, None] - upper[None, None, :, None]
        == charge_next[None, None, None, :]
    )
    masked_mps = jnp.where(keep_mps, mps_site, jnp.zeros_like(mps_site))
    keep_ket = (
        upper[:, None, None, None, None] + link_here[None, :, None, None, None]
        == lower[None, None, :, None, None]
        + link_next[None, None, None, :, None]
        + physical[None, None, None, None, :]
    )
    masked_ket = jnp.where(keep_ket, ket_site, jnp.zeros_like(ket_site))
    keep_left = (
        fresh_here[:, None, None, None]
        == charge_here[None, :, None, None]
        + link_here[None, None, :, None]
        - link_here[None, None, None, :]
    )
    masked_left = jnp.where(keep_left, left_site, jnp.zeros_like(left_site))
    keep_right = (
        charge_next[:, None, None, None]
        + link_next[None, :, None, None]
        - link_next[None, None, :, None]
        == fresh_next[None, None, None, :]
    )
    masked_right = jnp.where(keep_right, right_site, jnp.zeros_like(right_site))
    first = jnp.einsum(
        "xalm,auvb->xlmuvb", masked_left, masked_mps, preferred_element_type=jnp.float32
    ).astype(jnp.bfloat16)
    second = jnp.einsum(
        "xlmuvb,uldrp->xmvbdrp", first, masked_ket, preferred_element_type=jnp.float32
    ).astype(jnp.bfloat16)
    third = jnp.einsum(
        "xmvbdrp,vmesp->xbdres", second, masked_ket, preferred_element_type=jnp.float32
    ).astype(jnp.bfloat16)
    return jnp.einsum("xbdres,brsy->xdey", third, masked_right, preferred_element_type=jnp.float32)


def local(mps, ket, left_proj, right_proj, bond_charge, new_charge, link_charge, vert_charge):
    sites_here = mps.shape[0]
    half = left_proj.shape[1]
    full_mps = lax.all_gather(mps, "sec", axis=1, tiled=True)
    chi_full = full_mps.shape[1]
    legs = full_mps.shape[2]
    received = from_behind((bond_charge, new_charge, link_charge), COL, -1)
    bond_next = jnp.concatenate([bond_charge[1:], received[0]], axis=0)
    fresh_next = jnp.concatenate([new_charge[1:], received[1]], axis=0)
    link_next = jnp.concatenate([link_charge[1:], received[2]], axis=0)
    arrived = from_behind(right_proj, COL, -1)
    partial_next = jnp.concatenate([right_proj[1:], arrived], axis=0)
    right_next = gather_directly(partial_next, "sec", 4)
    offset = lax.axis_index("sec") * half
    fresh_half = lax.dynamic_slice_in_dim(new_charge[0], offset, half, 0)
    images = [
        absorb(
            full_mps[0],
            ket[0],
            left_proj[0],
            right_next[0],
            bond_charge[0],
            bond_next[0],
            fresh_half,
            fresh_next[0],
            link_charge[0],
            link_next[0],
            vert_charge[0],
        )
    ]
    image = jnp.stack(images, axis=0)
    partial_value = jnp.sum(image * image, axis=(1, 2, 3, 4))
    count = chi_full * legs * legs * chi_full
    columns = lax.axis_size(COL)
    squares = gathered_total(partial_value, "sec")
    meansq = squares / count
    logs = 0.5 * jnp.log(meansq + 1e-06)
    total = one_axis_at_a_time(jnp.sum(logs), COL)
    log_norm = total / (sites_here * columns)
    scale = lax.rsqrt(meansq + 1e-06)
    new_mps = (image * scale[:, None, None, None, None]).astype(jnp.bfloat16)
    return (new_mps, log_norm)


def solution(mesh):
    torus = Mesh(
        mesh.devices.reshape(4, 8, 4, mesh.shape["sec"]), ("col_0", "col_1", "col_2", "sec")
    )
    in_specs = (
        P(COL, "sec", None, None, None),
        P(COL, None, None, None, None, None),
        P(COL, "sec", None, None, None),
        P(COL, None, None, None, "sec"),
        P(COL, None),
        P(COL, None),
        P(COL, None),
        P(COL, None, None),
    )
    out_specs = (P(COL, "sec", None, None, None), P())
    return jax.shard_map(local, mesh=torus, in_specs=in_specs, out_specs=out_specs, check_vma=False)
```

profile of v0, /device:TPU:32, one launch (start us, length us, event | category | flops | bytes accessed | tf_op | source)
XLA Modules:
  0.0 162.3 jit_solution(1129275034538465947)
XLA Ops:
  0.6 2.6 %collective-permute-start = (s32[1,96]{1,0:T(1,128)}, s32[1,96]{1,0:T(1,128)S(1)}, u32[]{:S(2)}, u32[]{:S(2)}) collective-permute-start(s32[1,96]{1,0:T(1,128)} %param.12), channel_id=1, source_target_pairs={{0,254},{2,0},{4,2},{6,4},{8,6},{10,8},{12,10},{14,12},{16,14},{18... | collective-permute-start | bytes 1160 | tf_op jit(solution)/shard_map/ppermute | solution.py:13
  3.3 0.7 collective-permute-start.1
  4.0 0.4 collective-permute-start.3
  4.5 2.2 %collective-permute-start.2 = (s32[1,96]{1,0:T(1,128)}, s32[1,96]{1,0:T(1,128)S(1)}, u32[]{:S(2)}, u32[]{:S(2)}) collective-permute-start(s32[1,96]{1,0:T(1,128)} %param.13), channel_id=1, source_target_pairs={{0,254},{2,0},{4,2},{6,4},{8,6},{10,8},{12,10},{14,12},{16,14},{18... | collective-permute-start | bytes 1160 | tf_op jit(solution)/shard_map/ppermute | solution.py:13
  6.6 0.8 slice_bitcast_fusion
  7.4 0.7 broadcast_add_fusion.2
  8.1 0.7 broadcast_add_fusion.4
  8.8 0.1 broadcast_subtract_fusion.1
  8.9 0.7 dynamic-slice_bitcast_fusion
  9.6 0.7 broadcast_subtract_fusion.2
  10.4 4.4 %all_gather.9 = bf16[1,96,6,6,96]{4,1,3,2,0:T(8,128)(2,1)} all-gather(bf16[1,48,6,6,96]{4,1,3,2,0:T(8,128)(2,1)} %param.8), channel_id=1, replica_groups=mesh['col_0'=4,'col_1'=8,'col_2'=4,'sec'=2] {'sec'}, dimensions={1}, use_global_device_ids=true | all-gather | bytes 995328 | tf_op jit(solution)/shard_map/all_gather | solution.py:97
  14.7 1.3 dynamic-slice.1
  16.0 0.0 collective-permute-done.1
  16.0 0.1 broadcast_add_fusion.1
  16.1 1.1 fusion.29
  17.2 5.8 %convert_bitcast_fusion = bf16[48,6,6,6,6,96,1,1]{5,0,4,3,2,1,7,6:T(8,128)(2,1)S(1)} fusion(bf16[1,96,6,6,96]{4,1,3,2,0:T(8,128)(2,1)} %all_gather.9, s32[96]{0:T(128)S(1)} %bitcast.67, s32[96,6,6]{0,2,1:T(8,128)S(1)} %broadcast_subtract_fusion.1, bf16[1,48,96,6,6]{2,1,4,3,0:T(8,128)(2,1)} %param.10, s32[96,6,6]{0,2,1:T(8,128)S(1)} %broadcast_subtract_fusion.2, ...), kind=kOutput, calls=%fused_computation.8 | convolution fusion | flops 1153585152 | bytes 12967488 | tf_op jit(solution)/shard_map/xalm,auvb->xlmuvb/dot_general | solution.py:82
  23.1 28.1 %fusion = bf16[48,6,6,96,6,6,2,1]{3,5,6,4,2,1,0,7:T(8,128)(2,1)} fusion(bf16[48,6,6,6,6,96,1,1]{5,0,4,3,2,1,7,6:T(8,128)(2,1)S(1)} %convert_bitcast_fusion, bf16[6,6,6,6,2,1,1,1]{3,4,2,1,0,7,6,5:T(2,128)(2,1)S(1)} %fusion.29), kind=kOutput, calls=%fused_computation.1 | convolution fusion | flops 871907328 | bytes 35836992 | tf_op jit(solution)/shard_map/xlmuvb,uldrp->xmvbdrp/dot_general | solution.py:85
  51.1 38.6 %bitcast_convert_fusion.1 = bf16[48,96,6,6,6,6]{1,5,4,3,2,0:T(8,128)(2,1)} fusion(bf16[48,6,6,96,6,6,2,1]{3,5,6,4,2,1,0,7:T(8,128)(2,1)} %fusion, bf16[6,6,6,6,2,1,1,1]{3,4,2,1,0,7,6,5:T(2,128)(2,1)S(1)} %fusion.29), kind=kOutput, calls=%fused_computation.2 | convolution fusion | flops 865935360 | bytes 35836992 | tf_op jit(solution)/shard_map/xmvbdrp,vmesp->xbdres/dot_general | solution.py:88
  89.7 0.1 broadcast_add_fusion
  89.8 0.1 broadcast_subtract_fusion
  89.8 1.1 broadcast_in_dim.20
  91.0 4.5 %all_to_all.5 = bf16[2,1,96,6,6,48]{2,5,4,3,1,0:T(8,128)(2,1)S(1)} all-to-all(bf16[2,1,96,6,6,48]{2,5,4,3,1,0:T(8,128)(2,1)S(1)} %broadcast_in_dim.20), channel_id=1, replica_groups=mesh['col_0'=4,'col_1'=8,'col_2'=4,'sec'=2] {'sec'}, dimensions={0} | all-to-all | bytes 1327104 | tf_op jit(solution)/shard_map/all_to_all | solution.py:24
  95.5 0.1 copy.16
  95.6 0.0 collective-permute-done.2
  95.6 17.4 %multiply_reduce_fusion = (f32[]{:T(128)}, f32[48,6,6,96]{3,0,2,1:T(8,128)S(1)}) fusion(bf16[96,6,6,96]{0,3,2,1:T(8,128)(2,1)S(1)} %bitcast.60, s32[96,6,6]{0,2,1:T(8,128)S(1)} %broadcast_subtract_fusion, s32[96]{0:T(128)S(1)} %bitcast.70, bf16[48,96,6,6,6,6]{1,5,4,3,2,0:T(8,128)(2,1)} %bitcast_convert_fusion.1), kind=kOutput, calls=%fused_computation.15 | convolution fusion | flops 1147613184 | bytes 13285252 | tf_op jit(solution)/shard_map/xbdres,brsy->xdey/dot_general | solution.py:91
  112.9 1.4 dynamic-update-slice
  114.3 2.4 %all-reduce = f32[2]{0:T(128)S(1)} all-reduce(f32[2]{0:T(128)S(1)} %dynamic-update-slice), channel_id=1, replica_groups=mesh['col_0'=4,'col_1'=8,'col_2'=4,'sec'=2] {'sec'}, use_global_device_ids=true, to_apply=%add | all-reduce | flops 2 | bytes 16
  116.8 0.6 reduce.3
  118.1 9.3 %psum.21 = f32[]{:T(128)} all-reduce(f32[]{:T(128)S(6)} %mul.24), channel_id=1, replica_groups=mesh['col_0'=4,'col_1'=8,'col_2'=4,'sec'=2] {'col_0'}, use_global_device_ids=true, to_apply=%region_2.3 | all-reduce | flops 1 | bytes 8 | tf_op jit(solution)/shard_map/psum | solution.py:37
  127.4 20.9 %psum.22 = f32[]{:T(128)} all-reduce(f32[]{:T(128)} %psum.21), channel_id=1, replica_groups=mesh['col_0'=4,'col_1'=8,'col_2'=4,'sec'=2] {'col_1'}, use_global_device_ids=true, to_apply=%region_3.4 | all-reduce | flops 1 | bytes 8 | tf_op jit(solution)/shard_map/psum | solution.py:37
  148.3 11.4 %psum.23 = f32[]{:T(128)} all-reduce(f32[]{:T(128)} %psum.22), channel_id=1, replica_groups=mesh['col_0'=4,'col_1'=8,'col_2'=4,'sec'=2] {'col_2'}, use_global_device_ids=true, to_apply=%region_4.5 | all-reduce | flops 1 | bytes 8 | tf_op jit(solution)/shard_map/psum | solution.py:37
  159.7 0.8 fusion.21
  (4 shorter events, 0.0 us)
Async XLA Ops:
  0.6 16.6 %collective-permute-start = (s32[1,96]{1,0:T(1,128)}, s32[1,96]{1,0:T(1,128)S(1)}, u32[]{:S(2)}, u32[]{:S(2)}) collective-permute-start(s32[1,96]{1,0:T(1,128)} %param.12), channel_id=1, source_target_pairs={{0,254},{2,0},{4,2},{6,4},{8,6},{10,8},{12,10},{14,12},{16,14},{18... | collective-permute-start | bytes 1160 | tf_op jit(solution)/shard_map/ppermute | solution.py:13
  3.3 12.7 %collective-permute-start.1 = (s32[1,6]{1,0:T(1,128)}, s32[1,6]{1,0:T(1,128)S(1)}, u32[]{:S(2)}, u32[]{:S(2)}) collective-permute-start(s32[1,6]{1,0:T(1,128)} %param.14), channel_id=1, source_target_pairs={{0,254},{2,0},{4,2},{6,4},{8,6},{10,8},{12,10},{14,12},{16,14},{18... | collective-permute-start | bytes 80 | tf_op jit(solution)/shard_map/ppermute | solution.py:13
  4.0 85.8 %collective-permute-start.3 = (bf16[1,96,6,6,48]{1,4,3,2,0:T(8,128)(2,1)}, bf16[1,96,6,6,48]{1,4,3,2,0:T(8,128)(2,1)}, u32[]{:S(2)}, u32[]{:S(2)}) collective-permute-start(bf16[1,96,6,6,48]{1,4,3,2,0:T(8,128)(2,1)} %param.11), channel_id=1, source_target_pairs={{0,254},{2,0},{4,2},{6,4},{8,6},{10,8},{12,10},{14,12},{16,14},{18... | collective-permute-start | bytes 995336 | tf_op jit(solution)/shard_map/ppermute | solution.py:13
  4.5 91.1 %collective-permute-start.2 = (s32[1,96]{1,0:T(1,128)}, s32[1,96]{1,0:T(1,128)S(1)}, u32[]{:S(2)}, u32[]{:S(2)}) collective-permute-start(s32[1,96]{1,0:T(1,128)} %param.13), channel_id=1, source_target_pairs={{0,254},{2,0},{4,2},{6,4},{8,6},{10,8},{12,10},{14,12},{16,14},{18... | collective-permute-start | bytes 1160 | tf_op jit(solution)/shard_map/ppermute | solution.py:13
where the time goes:
time: 163 us; the launch traced here: 162 us
  matrix products  89.8 us (55%)
  blocking collectives  52.9 us (32%)
  starting transfers between devices  5.99 us (4%)
  local copies, waits for them, and re-layouts  5.34 us (3%)
  other arithmetic  5.05 us (3%)
  between operations  3.21 us (2%)
    psum x3, blocking collectives, one_axis_at_a_time(): return functools.reduce(lax.psum, axes, x)  41.6 us
    dot_general x1, matrix products, absorb(): jnp.einsum('xmvbdrp,vmesp->xbdres', second, masked_ket, preferred_element...  38.6 us
    dot_general x1, matrix products, absorb(): jnp.einsum('xlmuvb,uldrp->xmvbdrp', first, masked_ket, preferred_element_...  28.1 us
    dot_general x1, matrix products, absorb(): jnp.einsum('xbdres,brsy->xdey', third, masked_right, preferred_element_ty...  17.4 us
    ppermute x4, starting transfers between devices, from_behind(): return lax.ppermute(x, axis, [(i, (i + by) % count) for i in range(count)])  5.99 us
    dot_general x1, matrix products, absorb(): jnp.einsum('xalm,auvb->xlmuvb', masked_left, masked_mps, preferred_elemen...  5.81 us
    all_to_all x1, blocking collectives, copy_for_each(): lax.all_to_all(jnp.broadcast_to(x[None], (count, *x.shape)), axis, 0, 0,...  4.52 us
    all_gather x1, blocking collectives, local(): full_mps = lax.all_gather(mps, 'sec', axis=1, tiled=True)  4.38 us
  transfers between devices with their start and end apart: 4, of which 0 were waited for; matrix products, arithmetic and copies ran while one was open for 49% of the time, Pallas kernels for 0%

commit v1 on v0

--- a/solution.py
+++ b/solution.py
@@ -94,7 +94,9 @@
 def local(mps, ket, left_proj, right_proj, bond_charge, new_charge, link_charge, vert_charge):
     sites_here = mps.shape[0]
     half = left_proj.shape[1]
-    full_mps = lax.all_gather(mps, "sec", axis=1, tiled=True)
+    full_mps = jnp.concatenate(
+        lax.all_to_all(jnp.stack([mps] * lax.axis_size("sec")), "sec", 0, 0), axis=1
+    )
     chi_full = full_mps.shape[1]
     legs = full_mps.shape[2]
     received = from_behind((bond_charge, new_charge, link_charge), COL, -1)

time: 163 us -> 168 us (1.031)
  blocking collectives: 52.9 us -> 48.4 us
  other arithmetic: 5.05 us -> 9.43 us
  starting transfers between devices: 5.99 us -> 9.61 us
    all_gather x1 -> x0, blocking collectives: 4.38 us -> none  [local(): full_mps = lax.all_gather(mps, 'sec', axis=1, tiled=True)]
    all_to_all x0 -> x1, starting transfers between devices: none -> 3.55 us  [local(): lax.all_to_all(jnp.stack([mps] * lax.axis_size('sec')), 'sec', 0, 0)]
    dot_general x1, matrix products: 5.81 us -> 8.83 us  [absorb(): jnp.einsum('xalm,auvb->xlmuvb', masked_left, masked_mps, preferred_elemen...]
    another operation x0 -> x1, other arithmetic: none -> 2.27 us  [local(): jnp.stack([mps] * lax.axis_size('sec'))]
  transfers between devices with their start and end apart: 4 -> 5, of which waited for: 0 -> 0; matrix products, arithmetic and copies ran while one was open for 49% -> 51% of each run, Pallas kernels for 0% -> 0%
where the time goes in v1:
time: 168 us; the launch traced here: 167 us
  matrix products  91.3 us (54%)
  blocking collectives  48.4 us (29%)
  starting transfers between devices  9.61 us (6%)
  other arithmetic  9.43 us (6%)
  local copies, waits for them, and re-layouts  4.96 us (3%)
  between operations  3.23 us (2%)
    psum x3, blocking collectives, one_axis_at_a_time(): return functools.reduce(lax.psum, axes, x)  41.5 us
    dot_general x1, matrix products, absorb(): jnp.einsum('xmvbdrp,vmesp->xbdres', second, masked_ket, preferred_element...  38.6 us
    dot_general x1, matrix products, absorb(): jnp.einsum('xlmuvb,uldrp->xmvbdrp', first, masked_ket, preferred_element_...  26.5 us
    dot_general x1, matrix products, absorb(): jnp.einsum('xbdres,brsy->xdey', third, masked_right, preferred_element_ty...  17.4 us
    dot_general x1, matrix products, absorb(): jnp.einsum('xalm,auvb->xlmuvb', masked_left, masked_mps, preferred_elemen...  8.83 us
    ppermute x4, starting transfers between devices, from_behind(): return lax.ppermute(x, axis, [(i, (i + by) % count) for i in range(count)])  6.06 us
    all_to_all x1, blocking collectives, copy_for_each(): lax.all_to_all(jnp.broadcast_to(x[None], (count, *x.shape)), axis, 0, 0,...  4.43 us
    all_to_all x1, starting transfers between devices, local(): lax.all_to_all(jnp.stack([mps] * lax.axis_size('sec')), 'sec', 0, 0)  3.55 us
  transfers between devices with their start and end apart: 5, of which 0 were waited for; matrix products, arithmetic and copies ran while one was open for 51% of the time, Pallas kernels for 0%

profile of v1, /device:TPU:32, one launch (start us, length us, event | category | flops | bytes accessed | tf_op | source)
XLA Modules:
  0.0 166.9 jit_solution(8796686511866597362)
XLA Ops:
  0.6 2.6 %collective-permute-start = (s32[1,96]{1,0:T(1,128)}, s32[1,96]{1,0:T(1,128)S(1)}, u32[]{:S(2)}, u32[]{:S(2)}) collective-permute-start(s32[1,96]{1,0:T(1,128)} %param.12), channel_id=1, source_target_pairs={{0,254},{2,0},{4,2},{6,4},{8,6},{10,8},{12,10},{14,12},{16,14},{18... | collective-permute-start | bytes 1160 | tf_op jit(solution)/shard_map/ppermute | solution.py:13
  3.3 2.3 %pad_maximum_fusion = bf16[2,1,48,6,6,96]{5,2,4,3,1,0:T(8,128)(2,1)} fusion(bf16[1,1,48,6,6,96]{5,2,4,3,1,0:T(8,128)(2,1)} %bitcast.62), kind=kLoop, calls=%fused_computation.13 | loop fusion | flops 331776 | bytes 995328 | tf_op jit(solution)/shard_map/stack | solution.py:98
  5.5 3.6 %all-to-all-start = ((bf16[2,1,48,6,6,96]{5,2,4,3,1,0:T(8,128)(2,1)}), bf16[2,1,48,6,6,96]{5,2,4,3,1,0:T(8,128)(2,1)S(1)}, u32[]{:S(2)}, u32[]{:S(2)}) async-start(bf16[2,1,48,6,6,96]{5,2,4,3,1,0:T(8,128)(2,1)} %pad_maximum_fusion), calls=%async_computation | async-start | bytes 1769472 | tf_op jit(solution)/shard_map/all_to_all | solution.py:98
  9.1 0.8 collective-permute-start.1
  9.9 0.4 collective-permute-start.3
  10.4 2.2 %collective-permute-start.2 = (s32[1,96]{1,0:T(1,128)}, s32[1,96]{1,0:T(1,128)S(1)}, u32[]{:S(2)}, u32[]{:S(2)}) collective-permute-start(s32[1,96]{1,0:T(1,128)} %param.13), channel_id=1, source_target_pairs={{0,254},{2,0},{4,2},{6,4},{8,6},{10,8},{12,10},{14,12},{16,14},{18... | collective-permute-start | bytes 1160 | tf_op jit(solution)/shard_map/ppermute | solution.py:13
  12.5 0.8 dynamic-slice_bitcast_fusion
  13.3 0.8 slice_bitcast_fusion
  14.0 0.5 broadcast.215
  14.6 1.3 reduce.8
  15.9 0.1 add.141
  16.0 0.1 broadcast_subtract_fusion
  16.1 0.7 broadcast_add_fusion.3
  16.8 0.7 broadcast_add_fusion.4
  17.6 0.7 broadcast_subtract_fusion.2
  18.3 1.3 dynamic-slice.1
  19.7 1.1 fusion.24
  20.8 0.7 compare_select_fusion.1
  21.5 8.8 %convert_bitcast_fusion = bf16[48,6,6,6,6,96,1,1]{5,0,4,3,2,1,7,6:T(8,128)(2,1)} fusion(bf16[96,6,6,96,1,1]{3,0,2,1,5,4:T(8,128)(2,1)S(1)} %bitcast.60, bf16[1,48,96,6,6]{2,1,4,3,0:T(8,128)(2,1)} %param.10, s32[96,6,6]{0,2,1:T(8,128)S(1)} %broadcast_subtract_fusion.2, s32[48]{0:T(128)S(1)} %dynamic-slice_bitcast_fusion), kind=kOutput, calls=%fused_computation.8 | convolution fusion | flops 1152921600 | bytes 12953280 | tf_op jit(solution)/shard_map/xalm,auvb->xlmuvb/dot_general | solution.py:82
  30.4 26.5 %fusion = bf16[48,6,6,96,6,6,2,1]{3,5,6,4,2,1,0,7:T(8,128)(2,1)} fusion(bf16[48,6,6,6,6,96,1,1]{5,0,4,3,2,1,7,6:T(8,128)(2,1)} %convert_bitcast_fusion, bf16[6,6,6,6,2,1,1,1]{3,4,2,1,0,7,6,5:T(2,128)(2,1)S(1)} %fusion.24), kind=kOutput, calls=%fused_computation.1 | convolution fusion | flops 871907328 | bytes 35836992 | tf_op jit(solution)/shard_map/xlmuvb,uldrp->xmvbdrp/dot_general | solution.py:85
  56.9 38.6 %bitcast_convert_fusion.1 = bf16[48,96,6,6,6,6]{1,5,4,3,2,0:T(8,128)(2,1)} fusion(bf16[48,6,6,96,6,6,2,1]{3,5,6,4,2,1,0,7:T(8,128)(2,1)} %fusion, bf16[6,6,6,6,2,1,1,1]{3,4,2,1,0,7,6,5:T(2,128)(2,1)S(1)} %fusion.24), kind=kOutput, calls=%fused_computation.2 | convolution fusion | flops 865935360 | bytes 35836992 | tf_op jit(solution)/shard_map/xmvbdrp,vmesp->xbdres/dot_general | solution.py:88
  95.5 0.1 broadcast_subtract_fusion.1
  95.6 0.1 broadcast_in_dim.20
  95.7 4.4 %all_to_all.10 = bf16[2,1,96,6,6,48]{2,5,4,3,1,0:T(8,128)(2,1)S(1)} all-to-all(bf16[2,1,96,6,6,48]{2,5,4,3,1,0:T(8,128)(2,1)S(1)} %broadcast_in_dim.20), channel_id=1, replica_groups=mesh['col_0'=4,'col_1'=8,'col_2'=4,'sec'=2] {'sec'}, dimensions={0} | all-to-all | bytes 1327104 | tf_op jit(solution)/shard_map/all_to_all | solution.py:24
  100.2 17.4 %multiply_reduce_fusion = (f32[]{:T(128)}, f32[48,6,6,96]{3,0,2,1:T(8,128)S(1)}) fusion(bf16[96,6,6,96]{0,3,2,1:T(8,128)(2,1)S(1)} %bitcast.61, s32[96,6,6]{0,2,1:T(8,128)S(1)} %broadcast_subtract_fusion.1, s32[96]{0:T(128)S(1)} %bitcast.73, bf16[48,96,6,6,6,6]{1,5,4,3,2,0:T(8,128)(2,1)} %bitcast_convert_fusion.1), kind=kOutput, calls=%fused_computation.15 | convolution fusion | flops 1147613184 | bytes 13285252 | tf_op jit(solution)/shard_map/xbdres,brsy->xdey/dot_general | solution.py:91
  117.6 1.4 dynamic-update-slice
  119.0 2.4 %all-reduce = f32[2]{0:T(128)S(1)} all-reduce(f32[2]{0:T(128)S(1)} %dynamic-update-slice), channel_id=1, replica_groups=mesh['col_0'=4,'col_1'=8,'col_2'=4,'sec'=2] {'sec'}, use_global_device_ids=true, to_apply=%add | all-reduce | flops 2 | bytes 16
  121.4 0.6 reduce.3
  122.7 9.3 %psum.21 = f32[]{:T(128)} all-reduce(f32[]{:T(128)S(6)} %mul.24), channel_id=1, replica_groups=mesh['col_0'=4,'col_1'=8,'col_2'=4,'sec'=2] {'col_0'}, use_global_device_ids=true, to_apply=%region_2.3 | all-reduce | flops 1 | bytes 8 | tf_op jit(solution)/shard_map/psum | solution.py:37
  132.0 20.9 %psum.22 = f32[]{:T(128)} all-reduce(f32[]{:T(128)} %psum.21), channel_id=1, replica_groups=mesh['col_0'=4,'col_1'=8,'col_2'=4,'sec'=2] {'col_1'}, use_global_device_ids=true, to_apply=%region_3.4 | all-reduce | flops 1 | bytes 8 | tf_op jit(solution)/shard_map/psum | solution.py:37
  152.9 11.4 %psum.23 = f32[]{:T(128)} all-reduce(f32[]{:T(128)} %psum.22), channel_id=1, replica_groups=mesh['col_0'=4,'col_1'=8,'col_2'=4,'sec'=2] {'col_2'}, use_global_device_ids=true, to_apply=%region_4.5 | all-reduce | flops 1 | bytes 8 | tf_op jit(solution)/shard_map/psum | solution.py:37
  164.3 0.8 fusion.17
  (11 shorter events, 0.3 us)
Async XLA Ops:
  0.6 20.2 %collective-permute-start = (s32[1,96]{1,0:T(1,128)}, s32[1,96]{1,0:T(1,128)S(1)}, u32[]{:S(2)}, u32[]{:S(2)}) collective-permute-start(s32[1,96]{1,0:T(1,128)} %param.12), channel_id=1, source_target_pairs={{0,254},{2,0},{4,2},{6,4},{8,6},{10,8},{12,10},{14,12},{16,14},{18... | collective-permute-start | bytes 1160 | tf_op jit(solution)/shard_map/ppermute | solution.py:13
  5.5 15.3 %all-to-all-start = ((bf16[2,1,48,6,6,96]{5,2,4,3,1,0:T(8,128)(2,1)}), bf16[2,1,48,6,6,96]{5,2,4,3,1,0:T(8,128)(2,1)S(1)}, u32[]{:S(2)}, u32[]{:S(2)}) async-start(bf16[2,1,48,6,6,96]{5,2,4,3,1,0:T(8,128)(2,1)} %pad_maximum_fusion), calls=%async_computation | async-start | bytes 1769472 | tf_op jit(solution)/shard_map/all_to_all | solution.py:98
  9.1 10.5 %collective-permute-start.1 = (s32[1,6]{1,0:T(1,128)}, s32[1,6]{1,0:T(1,128)S(1)}, u32[]{:S(2)}, u32[]{:S(2)}) collective-permute-start(s32[1,6]{1,0:T(1,128)} %param.14), channel_id=1, source_target_pairs={{0,254},{2,0},{4,2},{6,4},{8,6},{10,8},{12,10},{14,12},{16,14},{18... | collective-permute-start | bytes 80 | tf_op jit(solution)/shard_map/ppermute | solution.py:13
  9.9 85.7 %collective-permute-start.3 = (bf16[1,96,6,6,48]{1,4,3,2,0:T(8,128)(2,1)}, bf16[1,96,6,6,48]{1,4,3,2,0:T(8,128)(2,1)S(1)}, u32[]{:S(2)}, u32[]{:S(2)}) collective-permute-start(bf16[1,96,6,6,48]{1,4,3,2,0:T(8,128)(2,1)} %param.11), channel_id=1, source_target_pairs={{0,254},{2,0},{4,2},{6,4},{8,6},{10,8},{12,10},{14,12},{16,14},{18... | collective-permute-start | bytes 995336 | tf_op jit(solution)/shard_map/ppermute | solution.py:13
  10.4 89.8 %collective-permute-start.2 = (s32[1,96]{1,0:T(1,128)}, s32[1,96]{1,0:T(1,128)S(1)}, u32[]{:S(2)}, u32[]{:S(2)}) collective-permute-start(s32[1,96]{1,0:T(1,128)} %param.13), channel_id=1, source_target_pairs={{0,254},{2,0},{4,2},{6,4},{8,6},{10,8},{12,10},{14,12},{16,14},{18... | collective-permute-start | bytes 1160 | tf_op jit(solution)/shard_map/ppermute | solution.py:13
